TPU v7x, 32 devices: a whole 2x2x4 slice. The times are simulated.
32 devices in a mesh: seq: 8 (over z, x), head: 4 (over y, core).
Axes of the slice: x: 2, y: 2, z: 4, core: 2. Of those that a mesh axis runs over, the one named last changes fastest.
Arguments:
- queries: bfloat16 [8192, 4096], P('seq', 'head'), may hold values from -8 to 8
- key_rows: bfloat16 [8192, 4096], P('seq', 'head'), may hold values from -8 to 8
- value_rows: bfloat16 [8192, 4096], P('seq', 'head'), may hold values from -6 to 6
- random_owner: int32 [128, 3], P('seq'), may hold values from 0 to 7, all different within a row; in each aligned block of 16 rows (0 to 15, 16 to 31, ...) at most 8 rows name the same one
- random_local: int32 [128, 3], P('seq'), may hold values from 0 to 15
- output_weight: bfloat16 [4096, 4096], P('head'), may hold values from -0.09375 to 0.09375
Outputs:
- layer_output: bfloat16 [8192, 4096], P(('seq', 'head'))
Inputs may be any that keep to these rules, and one draw needn't show every extreme that they name: `random_owner`: each row names 3 different owners. Among the rows of one device (16 aligned rows) no owner is named more than 8 times, and in some device's rows one owner is named exactly 8 times.
All inputs are finite; a program needn't handle non-finite values.
Results may differ from a plain program's by a relative error of at most 0.0052.
Values may be sent and summed in bfloat16 or wider, within the bound.
No kernel may reach another device: no remote copies, remote signals or barrier semaphores. Data moves between devices by JAX's collectives and lax.ppermute only.
A program may use at most 192 MiB of HBM per device.

v0:
```python
import math
import jax
import jax.numpy as jnp
from jax import lax
from jax.sharding import PartitionSpec as P

HEAD_DIM = 128
BLOCK = 64
RANDOM = 3
GLOBAL = 128
masked_score = -1e30


def padded(array, sides, width):
    for axis, dim in sides:
        peers, length = (lax.axis_size(axis), array.shape[dim])
        up = [(i, (i + 1) % peers) for i in range(peers - 1)]
        down = [(j, i) for i, j in up]
        last = lax.slice_in_dim(array, length - width, length, axis=dim)
        first = lax.slice_in_dim(array, 0, width, axis=dim)
        before = lax.ppermute(last, axis, up)
        after = lax.ppermute(first, axis, down)
        array = jnp.concatenate([before, array, after], axis=dim)
    return array


def from_root(block, axis, holder):
    block = jnp.where(lax.axis_index(axis) == holder, block, jnp.zeros_like(block))
    return lax.psum(block, axis)


def combined_all(array, axis, combine):
    everything = jax.tree.map(lambda part: lax.all_gather(part, axis), array)
    first = jax.tree.map(lambda part: part[0], everything)

    def lap(k, so_far):
        return combine(so_far, jax.tree.map(lambda part: part[k], everything))

    return lax.fori_loop(1, lax.axis_size(axis), lap, first)


def slot_table(owner_ids, local_ids, seq_count, slot_count):
    owner_hits = (owner_ids[:, None] == jnp.arange(seq_count, dtype=jnp.int32)[None, :]).astype(
        jnp.int32
    )
    earlier = jnp.cumsum(owner_hits, axis=0) - owner_hits
    slot_ids = jnp.sum(earlier * owner_hits, axis=1)
    slot_hits = (slot_ids[:, None] == jnp.arange(slot_count, dtype=jnp.int32)[None, :]).astype(
        jnp.int32
    )
    request_table = jnp.sum(
        (owner_hits * local_ids[:, None])[:, :, None] * slot_hits[:, None, :], axis=0
    )
    return (request_table, slot_ids)


def local(queries, key_rows, value_rows, random_owner, random_local, output_weight):
    seq_count = lax.axis_size("seq")
    seq_index = lax.axis_index("seq")
    token_count, width_here = queries.shape
    blocks_here = token_count // BLOCK
    heads_here = width_here // HEAD_DIM
    slot_count = max(2, 4 * blocks_here // seq_count)
    total_blocks = seq_count * blocks_here
    score_scale = HEAD_DIM ** (-0.5)
    key_blocks = key_rows.reshape(blocks_here, BLOCK, width_here)
    value_blocks = value_rows.reshape(blocks_here, BLOCK, width_here)
    edge_slots = 0
    owner_flat = random_owner.reshape(-1)
    local_flat = random_local.reshape(-1)
    request_table, slot_ids = slot_table(owner_flat, local_flat, seq_count, slot_count)
    wanted = lax.all_to_all(request_table, "seq", split_axis=0, concat_axis=0, tiled=True)
    sent_keys = jnp.take(key_blocks, wanted, axis=0)
    sent_values = jnp.take(value_blocks, wanted, axis=0)
    got_keys = lax.all_to_all(sent_keys, "seq", split_axis=0, concat_axis=0, tiled=True)
    got_values = lax.all_to_all(sent_values, "seq", split_axis=0, concat_axis=0, tiled=True)
    slot_width = slot_count + edge_slots
    flat_slots = owner_flat * slot_width + slot_ids
    random_keys = jnp.take(got_keys.reshape(-1, BLOCK, width_here), flat_slots, axis=0)
    random_values = jnp.take(got_values.reshape(-1, BLOCK, width_here), flat_slots, axis=0)
    edge_pairs = jnp.stack(
        [jnp.stack([key_blocks[0], value_blocks[0]]), jnp.stack([key_blocks[-1], value_blocks[-1]])]
    )
    widened = padded(edge_pairs, (("seq", 0),), 1)
    left_key, left_value = (widened[0, 0], widened[0, 1])
    right_key, right_value = (widened[3, 0], widened[3, 1])
    global_rows = jnp.stack([queries[:GLOBAL], key_rows[:GLOBAL], value_rows[:GLOBAL]])
    global_rows = from_root(global_rows, "seq", 0)
    global_query = global_rows[0].reshape(GLOBAL, heads_here, HEAD_DIM)
    key_heads = key_rows.reshape(token_count, heads_here, HEAD_DIM)
    value_heads = value_rows.reshape(token_count, heads_here, HEAD_DIM)
    scores = (
        jnp.einsum("qhd,khd->hqk", global_query, key_heads, preferred_element_type=jnp.float32)
        * score_scale
    )
    row_max = jnp.max(scores, axis=2)
    weight = jnp.exp(scores - row_max[:, :, None])
    row_total = jnp.sum(weight, axis=2)
    partial_value = jnp.einsum(
        "hqk,khd->hqd", weight.astype(jnp.bfloat16), value_heads, preferred_element_type=jnp.float32
    )

    def combine(left_part, right_part):
        joint_max = jnp.maximum(left_part[0], right_part[0])
        left_factor = jnp.exp(left_part[0] - joint_max)
        right_factor = jnp.exp(right_part[0] - joint_max)
        return (
            joint_max,
            left_part[1] * left_factor + right_part[1] * right_factor,
            left_part[2] * left_factor[:, :, None] + right_part[2] * right_factor[:, :, None],
        )

    row_max, row_total, partial_value = combined_all(
        (row_max, row_total, partial_value), "seq", combine
    )
    global_out = jnp.transpose(partial_value / row_total[:, :, None], (1, 0, 2)).reshape(
        GLOBAL, width_here
    )
    key_padded = jnp.concatenate([left_key[None], key_blocks, right_key[None]], axis=0)
    value_padded = jnp.concatenate([left_value[None], value_blocks, right_value[None]], axis=0)
    global_keys = global_rows[1].reshape(GLOBAL // BLOCK, BLOCK, width_here)
    global_values = global_rows[2].reshape(GLOBAL // BLOCK, BLOCK, width_here)
    group_size = math.gcd(blocks_here, max(1, 512 // BLOCK))
    group_count = blocks_here // group_size
    listed = (3 + RANDOM) * BLOCK + GLOBAL
    slot_number = jnp.arange(listed, dtype=jnp.int32) // BLOCK

    def attend(packed):
        number, query_group, key_group, value_group = packed
        block_ids = (
            seq_index * blocks_here + number * group_size + jnp.arange(group_size, dtype=jnp.int32)
        )
        near_keys = lax.dynamic_slice_in_dim(key_padded, number * group_size, group_size + 2, 0)
        near_values = lax.dynamic_slice_in_dim(value_padded, number * group_size, group_size + 2, 0)
        window_keys = jnp.stack([near_keys[:-2], near_keys[1:-1], near_keys[2:]], axis=1)
        window_values = jnp.stack([near_values[:-2], near_values[1:-1], near_values[2:]], axis=1)
        listed_keys = jnp.concatenate(
            [
                window_keys,
                key_group,
                jnp.broadcast_to(global_keys[None], (group_size,) + global_keys.shape),
            ],
            axis=1,
        )
        listed_values = jnp.concatenate(
            [
                window_values,
                value_group,
                jnp.broadcast_to(global_values[None], (group_size,) + global_values.shape),
            ],
            axis=1,
        )
        group_keys = listed_keys.reshape(group_size, listed, heads_here, HEAD_DIM)
        group_values = listed_values.reshape(group_size, listed, heads_here, HEAD_DIM)
        query_heads = query_group.reshape(group_size, BLOCK, heads_here, HEAD_DIM)
        block_scores = (
            jnp.einsum(
                "bqhd,bkhd->bhqk", query_heads, group_keys, preferred_element_type=jnp.float32
            )
            * score_scale
        )
        usable = jnp.logical_and(
            jnp.logical_or(slot_number[None, :] != 0, block_ids[:, None] > 0),
            jnp.logical_or(slot_number[None, :] != 2, block_ids[:, None] < total_blocks - 1),
        )
        usable_keys = usable[:, None, None, :]
        block_scores = jnp.where(usable_keys, block_scores, masked_score)
        block_max = jnp.max(block_scores, axis=3, keepdims=True)
        block_weight = jnp.where(usable_keys, jnp.exp(block_scores - block_max), 0.0)
        block_total = jnp.sum(block_weight, axis=3)
        context = jnp.einsum(
            "bhqk,bkhd->bqhd",
            block_weight.astype(jnp.bfloat16),
            group_values,
            preferred_element_type=jnp.float32,
        )
        context = context / jnp.transpose(block_total, (0, 2, 1))[:, :, :, None]
        return context.reshape(group_size * BLOCK, width_here).astype(jnp.bfloat16)

    numbers = jnp.arange(group_count, dtype=jnp.int32)
    query_groups = queries.reshape(group_count, group_size, BLOCK, width_here)
    random_key_groups = random_keys.reshape(group_count, group_size, RANDOM, BLOCK, width_here)
    random_value_groups = random_values.reshape(group_count, group_size, RANDOM, BLOCK, width_here)
    sparse = lax.map(
        attend, (numbers, query_groups, random_key_groups, random_value_groups)
    ).reshape(token_count, width_here)
    top_rows = jnp.where(seq_index == 0, global_out.astype(jnp.bfloat16), sparse[:GLOBAL])
    attention = jnp.concatenate([top_rows, sparse[GLOBAL:]], axis=0)
    summed = lax.psum_scatter(
        jnp.dot(attention, output_weight, preferred_element_type=jnp.float32),
        "head",
        scatter_dimension=0,
        tiled=True,
    )
    return summed.astype(jnp.bfloat16)


def solution(mesh):
    in_specs = (
        P("seq", "head"),
        P("seq", "head"),
        P("seq", "head"),
        P("seq", None),
        P("seq", None),
        P("head", None),
    )
    out_specs = P(("seq", "head"), None)
    return jax.shard_map(local, mesh=mesh, in_specs=in_specs, out_specs=out_specs, check_vma=False)
```

profile of v0, /device:TPU:0, one launch (start us, length us, event | category | flops | bytes accessed | tf_op | source)
XLA Modules:
  0.0 904.8 jit_solution(16662353208190921498)
XLA Ops:
  8.9 13.6 %all_to_all.22 = s32[8,1,8]{2,1,0:T(1,128)S(1)} all-to-all(s32[8,1,8]{2,1,0:T(1,128)S(1)} %bitcast.212), channel_id=1, replica_groups=mesh['seq'=8,'head'=4] {'seq'}, dimensions={0} | all-to-all | bytes 512 | tf_op jit(solution)/shard_map/all_to_all | solution.py:72
  22.6 7.2 gather_fusion
  29.8 5.5 gather_fusion.2
  35.3 9.4 %broadcast_select_fusion = (bf16[8,8,64,1024]{3,2,1,0:T(8,128)(2,1)}, bf16[8,8,64,1024]{3,2,1,0:T(8,128)(2,1)S(1)}) fusion(bf16[8,8,64,1024]{3,2,1,0:T(8,128)(2,1)} %bitcast.198, pred[8,8]{1,0:T(8,128)(4,1)S(1)} %compare_and_fusion, bf16[8,8,64,1024]{3,2,1,0:T(8,128)(2,1)} %bitcast.197), kind=kLoop, calls=%fused_computation.61 | loop fusion | flops 8388608 | bytes 33554496 | tf_op jit(solution)/shard_map/jit(_take)/select_n | solution.py:73
  44.7 185.8 %all_to_all.23 = bf16[8,8,64,1024]{3,2,1,0:T(8,128)(2,1)} all-to-all(bf16[8,8,64,1024]{3,2,1,0:T(8,128)(2,1)S(1)} %get-tuple-element.475), channel_id=1, replica_groups=mesh['seq'=8,'head'=4] {'seq'}, dimensions={0} | all-to-all | bytes 16777216 | tf_op jit(solution)/shard_map/all_to_all | solution.py:76
  230.5 5.2 all-to-all-start.2
  238.3 228.5 %all-reduce.2.cloned.1.call-done = bf16[3,128,1024]{1,2,0:T(8,128)(2,1)} async-done(((bf16[3,128,1024]{1,2,0:T(8,128)(2,1)}), bf16[3,128,1024]{1,2,0:T(8,128)(2,1)}) %all-reduce.2.cloned.1.call-update) | async-done | bytes 786448 | tf_op jit(solution)/shard_map/psum | solution.py:29
  474.1 2.6 collective-permute-start
  478.1 11.4 %collective-permute-done = bf16[1,2,64,1024]{3,2,1,0:T(8,128)(2,1)S(1)} collective-permute-done((bf16[1,2,64,1024]{3,2,1,0:T(8,128)(2,1)S(1)}, bf16[1,2,64,1024]{3,2,1,0:T(8,128)(2,1)S(1)}, u32[]{:S(2)}, u32[]{:S(2)}) %collective-permute-start) | collective-permute-done | bytes 262176 | tf_op jit(solution)/shard_map/ppermute | solution.py:21
  494.9 33.3 %all-gather.1 = f32[64,128]{1,0:T(8,128)S(1)} all-gather(f32[8,128]{1,0:T(8,128)S(1)} %fusion.37), channel_id=3, replica_groups=mesh['seq'=8,'head'=4] {'seq'}, dimensions={0}, use_global_device_ids=true | all-gather | bytes 36864 | tf_op jit(solution)/shard_map/all_gather | solution.py:33
  528.2 31.3 %all-gather = f32[64,128]{1,0:T(8,128)S(1)} all-gather(f32[8,128]{1,0:T(8,128)S(1)} %get-tuple-element.480), channel_id=2, replica_groups=mesh['seq'=8,'head'=4] {'seq'}, dimensions={0}, use_global_device_ids=true | all-gather | bytes 36864 | tf_op jit(solution)/shard_map/all_gather | solution.py:33
  562.3 11.0 %while.33 = (s32[]{:T(128)}, f32[8,128]{1,0:T(8,128)S(1)}, f32[8,128]{1,0:T(8,128)S(1)}, f32[8,128,128]{2,1,0:T(8,128)S(1)}, f32[8,8,128]{2,1,0:T(8,128)S(1)}, /...) while((s32[]{:T(128)}, f32[8,128]{1,0:T(8,128)S(1)}, ...), condition=%wide.region_4.5_spmd, body=%wide.region_3.4_spmd.sunk | while | flops 399365 | bytes 1613975 | solution.py:39
  574.2 8.4 gather_fusion.1
  582.6 8.4 gather_fusion.3
  591.0 10.4 %broadcast_select_fusion.2 = (bf16[48,64,1024]{2,1,0:T(8,128)(2,1)}, bf16[48,64,1024]{2,1,0:T(8,128)(2,1)}) fusion(bf16[48,64,1024]{2,1,0:T(8,128)(2,1)} %gather_fusion.3, pred[48]{0:T(512)(128)(4,1)S(1)} %get-tuple-element.453, bf16[48,64,1024]{2,1,0:T(8,128)(2,1)} %gather_fusion.1), kind=kLoop, calls=%fused_computation.63 | loop fusion | flops 6291456 | bytes 25165872 | tf_op jit(solution)/shard_map/jit(_take)/select_n | solution.py:79
  601.4 146.4 %while.34 = (s32[]{:T(128)}, bf16[2,512,1024]{2,1,0:T(8,128)(2,1)}, s32[2]{0:T(128)S(1)}, bf16[18,64,1024]{2,1,0:T(8,128)(2,1)S(1)}, bf16[2,8,3,64,1024]{4,3,2,1...) while((s32[]{:T(128)}, bf16[2,512,1024]{2,1,0:T(8,128)(2,1)}, ...), condition=%wide.region_11.14_spmd.clone.clone, body=%wide.region_8.13_spmd.clone.clone.sunk | while | flops 1091585536 | bytes 126397792 | solution.py:184
  612.6 6.7 bitcast_dynamic-update-slice_fusion.3
  619.3 2.5 broadcast_dynamic-update-slice_fusion.5
  621.8 8.9 copy.127
  631.2 9.6 %fusion.93 = f32[8,8,64,512]{3,2,1,0:T(8,128)} fusion(bf16[8,512,8,128]{3,2,1,0:T(8,128)(2,1)} %bitcast.186, bf16[8,64,8,128]{3,2,1,0:T(8,128)(2,1)S(1)} %bitcast.189), kind=kOutput, calls=%fused_computation.16.clone.1 | convolution fusion | flops 536870912 | bytes 17825792 | tf_op jit(solution)/shard_map/while/body/eval_jaxpr/bqhd,bkhd->bhqk/dot_general | solution.py:157
  640.9 11.5 %fusion.96 = (f32[8,8,64]{2,1,0:T(8,128)S(1)}, bf16[8,8,64,512]{3,2,1,0:T(8,128)(2,1)}) fusion(f32[8,8,64,512]{3,2,1,0:T(8,128)} %fusion.93, pred[8,512]{1,0:T(8,128)(4,1)S(1)} %or_and_fusion.2), kind=kOutput, calls=%fused_computation.111.clone.1 | output fusion | flops 16777728 | bytes 12603392 | tf_op jit(solution)/shard_map/while/body/eval_jaxpr/sub | solution.py:169
  654.9 8.8 copy.126
  663.7 6.6 fusion.97
  685.8 6.7 bitcast_dynamic-update-slice_fusion.3
  695.0 8.9 copy.127
  704.4 9.6 %fusion.93 = f32[8,8,64,512]{3,2,1,0:T(8,128)} fusion(bf16[8,512,8,128]{3,2,1,0:T(8,128)(2,1)} %bitcast.186, bf16[8,64,8,128]{3,2,1,0:T(8,128)(2,1)S(1)} %bitcast.189), kind=kOutput, calls=%fused_computation.16.clone.1 | convolution fusion | flops 536870912 | bytes 17825792 | tf_op jit(solution)/shard_map/while/body/eval_jaxpr/bqhd,bkhd->bhqk/dot_general | solution.py:157
  714.1 11.5 %fusion.96 = (f32[8,8,64]{2,1,0:T(8,128)S(1)}, bf16[8,8,64,512]{3,2,1,0:T(8,128)(2,1)}) fusion(f32[8,8,64,512]{3,2,1,0:T(8,128)} %fusion.93, pred[8,512]{1,0:T(8,128)(4,1)S(1)} %or_and_fusion.2), kind=kOutput, calls=%fused_computation.111.clone.1 | output fusion | flops 16777728 | bytes 12603392 | tf_op jit(solution)/shard_map/while/body/eval_jaxpr/sub | solution.py:169
  728.1 8.8 copy.126
  736.9 6.6 fusion.97
  753.1 16.1 %fusion.45 = f32[1024,4096]{1,0:T(8,128)} fusion(bf16[1024,4096]{1,0:T(8,128)(2,1)} %param.19, bf16[896,1024]{0,1:T(8,128)(2,1)} %copy.92, bf16[128,1024]{0,1:T(8,128)(2,1)S(1)} %bitcast_select_fusion), kind=kOutput, calls=%fused_computation.77 | convolution fusion | flops 8594128896 | bytes 27262976 | tf_op jit(solution)/shard_map/dot_general | solution.py:190
  769.3 125.2 %reduce-scatter.2.cloned.1.call-done = f32[256,4096]{1,0:T(8,128)} async-done(((f32[1024,4096]{1,0:T(8,128)}), f32[256,4096]{1,0:T(8,128)}) %reduce-scatter.2.cloned.1.call-update) | async-done | bytes 4194320 | tf_op jit(solution)/shard_map/reduce_scatter | solution.py:189
  894.5 3.8 convert_element_type.51
  (123 shorter events, 77.1 us)
Async XLA Ops:
  22.5 7.3 copy-start
  230.5 6.2 slice-start
  230.5 352.1 %all-to-all-start.2 = ((bf16[8,8,64,1024]{3,2,1,0:T(8,128)(2,1)}), bf16[8,8,64,1024]{3,2,1,0:T(8,128)(2,1)}, u32[]{:S(2)}, u32[]{:S(2)}) async-start(bf16[8,8,64,1024]{3,2,1,0:T(8,128)(2,1)} %get-tuple-element.474), calls=%async_computation.2 | async-start | bytes 16777216 | tf_op jit(solution)/shard_map/all_to_all | solution.py:75
  235.7 231.1 %all-reduce.2.cloned.1.call-start = ((), (), s32[]{:S(2)}) async-start(), calls=%async_computation.4 | async-start | bytes 1572864 | tf_op jit(solution)/shard_map/psum | solution.py:29
  238.3 322.9 %all-gather.5.cloned.1.call-start = ((), (), s32[]{:S(2)}) async-start(), calls=%async_computation.6 | async-start | bytes 4718592 | tf_op jit(solution)/shard_map/all_gather | solution.py:33
  466.8 4.1 copy-start.2
  469.0 1.9 copy-start.3
  473.0 421.5 %reduce-scatter.2.cloned.1.call-start = ((), (), s32[]{:S(2)}) async-start(), calls=%async_computation.5 | async-start | bytes 20971520 | tf_op jit(solution)/shard_map/reduce_scatter | solution.py:189
  474.1 15.4 %collective-permute-start = (bf16[1,2,64,1024]{3,2,1,0:T(8,128)(2,1)S(1)}, bf16[1,2,64,1024]{3,2,1,0:T(8,128)(2,1)S(1)}, u32[]{:S(2)}, u32[]{:S(2)}) collective-permute-start(bf16[1,2,64,1024]{3,2,1,0:T(8,128)(2,1)S(1)} %maximum_bitcast_fusion), channel_id=1, source_target_pairs={{0,4},{4,8},{8,12},{12,16},{16,20},{20,24},{24,28},{1,5},{5,9},{9,... | collective-permute-start | bytes 786440 | tf_op jit(solution)/shard_map/ppermute | solution.py:21
  476.8 13.6 %collective-permute-start.1 = (bf16[1,2,64,1024]{3,2,1,0:T(8,128)(2,1)S(1)}, bf16[1,2,64,1024]{3,2,1,0:T(8,128)(2,1)S(1)}, u32[]{:S(2)}, u32[]{:S(2)}) collective-permute-start(bf16[1,2,64,1024]{3,2,1,0:T(8,128)(2,1)S(1)} %maximum_bitcast_fusion.1), channel_id=1, source_target_pairs={{4,0},{8,4},{12,8},{16,12},{20,16},{24,20},{28,24},{5,1},{9,5},{13... | collective-permute-start | bytes 786440 | tf_op jit(solution)/shard_map/ppermute | solution.py:22
  478.1 14.2 %copy-start.1 = (bf16[1024,1024]{1,0:T(8,128)(2,1)S(1)}, bf16[1024,1024]{1,0:T(8,128)(2,1)}, u32[]{:S(2)}) copy-start(bf16[1024,1024]{1,0:T(8,128)(2,1)} %param.15) | copy-start | bytes 6291460
  478.1 15.9 %copy-start.4 = (f32[8,128,1024]{2,1,0:T(8,128)S(1)}, f32[8,128,1024]{2,1,0:T(8,128)}, u32[]{:S(2)}) copy-start(f32[8,128,1024]{2,1,0:T(8,128)} %copy-done.3) | copy-start | bytes 12582916
  621.8 8.9 copy-start.5
  695.0 8.9 copy-start.5
  747.8 5.3 copy-start.6
Sparse Core Ops, SparseCore 0:
  239.9 226.8 all-reduce.1
  473.1 75.0 all-gather.4
  769.4 125.0 reduce-scatter.1
where the time goes:
time: 906 us; the launch traced here: 905 us
  waiting for transfers between devices  366 us (40%)
  blocking collectives  264 us (29%)
  local copies, waits for them, and re-layouts  135 us (15%)
  other arithmetic  64.4 us (7%)
  matrix products  51.6 us (6%)
  between operations  13.4 us (1%)
  starting transfers between devices  9.2 us (1%)
    psum x1, waiting for transfers between devices, from_root(): return lax.psum(block, axis)  228 us
    all_to_all x1, blocking collectives, local(): lax.all_to_all(sent_values, 'seq', split_axis=0, concat_axis=0, tiled=True)  186 us
    reduce_scatter x1, waiting for transfers between devices, local(): lax.psum_scatter(jnp.dot(attention, output_weight, preferred_element_type...  125 us
    while x24, local copies, waits for them, and re-layouts  69.2 us
    all_gather x2, blocking collectives, combined_all(): everything = jax.tree.map(lambda part: lax.all_gather(part, axis), array)  64.6 us
    sub x2, other arithmetic, attend(): block_scores - block_max  23 us
    dot_general x2, matrix products, attend(): jnp.einsum('bqhd,bkhd->bhqk', query_heads, group_keys, preferred_element_...  19.3 us
  transfers between devices with their start and end apart: 6, of which 4 were waited for; matrix products, arithmetic and copies ran while one was open for 4% of the time, Pallas kernels for 0%

commit v1 on v0

--- a/solution.py
+++ b/solution.py
@@ -9,6 +9,40 @@
 RANDOM = 3
 GLOBAL = 128
 masked_score = -1e30
+
+
+def arrange_node(load, in_dim, shard_in):
+    piece_now = load.shape
+    a_next = load.reshape(
+        *piece_now[:in_dim], shard_in, piece_now[in_dim] // shard_in, *piece_now[in_dim + 1 :]
+    )
+    current_value = jnp.moveaxis(a_next, in_dim, 0)
+    return current_value
+
+
+def write_zones(sheet, pos_dim):
+    sheet = jnp.moveaxis(sheet, 0, pos_dim)
+    z1 = sheet.shape
+    x_next = sheet.reshape(*z1[:pos_dim], z1[pos_dim] * z1[pos_dim + 1], *z1[pos_dim + 2 :])
+    return x_next
+
+
+def step_on_side(mesh_name, body, piece_in, slab_in):
+    parts_out = lax.axis_size(mesh_name)
+    known = lax.axis_index(mesh_name)
+    o_now, w1 = (parts_out, known)
+    part_next = arrange_node(body, piece_in, o_now)
+    fresh = part_next
+    for c in range(1, o_now):
+        prior, h_now = ((w1 + c) % o_now, (w1 - c) % o_now)
+        d_next = lax.dynamic_index_in_dim(part_next, prior, 0)
+        arr_out = range(o_now)
+        w2 = map(lambda nth: (nth, (nth + c) % o_now), arr_out)
+        kept_arr = list(w2)
+        block_next = lax.ppermute(d_next, mesh_name, kept_arr)
+        fresh = lax.dynamic_update_slice_in_dim(fresh, block_next, h_now, axis=0)
+    spare = write_zones(fresh, slab_in)
+    return spare
 
 
 def padded(array, sides, width):
@@ -73,7 +107,7 @@
     sent_keys = jnp.take(key_blocks, wanted, axis=0)
     sent_values = jnp.take(value_blocks, wanted, axis=0)
     got_keys = lax.all_to_all(sent_keys, "seq", split_axis=0, concat_axis=0, tiled=True)
-    got_values = lax.all_to_all(sent_values, "seq", split_axis=0, concat_axis=0, tiled=True)
+    got_values = step_on_side("seq", sent_values, 0, 0)
     slot_width = slot_count + edge_slots
     flat_slots = owner_flat * slot_width + slot_ids
     random_keys = jnp.take(got_keys.reshape(-1, BLOCK, width_here), flat_slots, axis=0)

time: 906 us -> 953 us (1.052)
  blocking collectives: 264 us -> 233 us
  starting transfers between devices: 9.2 us -> 36.3 us
  local copies, waits for them, and re-layouts: 135 us -> 160 us
  waiting for transfers between devices: 366 us -> 387 us
    all_to_all x1 -> x0, blocking collectives: 186 us -> none  [local(): lax.all_to_all(sent_values, 'seq', split_axis=0, concat_axis=0, tiled=True)]
    all_gather x2, blocking collectives: 64.6 us -> 219 us  [combined_all(): everything = jax.tree.map(lambda part: lax.all_gather(part, axis), array)]
    ppermute x0 -> x7, starting transfers between devices: none -> 27.1 us  [step_on_side(): block_next = lax.ppermute(d_next, mesh_name, kept_arr)]
    ppermute x0 -> x7, waiting for transfers between devices: none -> 21.2 us  [step_on_side(): block_next = lax.ppermute(d_next, mesh_name, kept_arr)]
    dynamic_update_slice x0 -> x7, local copies, waits for them, and re-layouts: none -> 16 us  [step_on_side(): fresh = lax.dynamic_update_slice_in_dim(fresh, block_next, h_now, axis=0)]
    ppermute x1, waiting for transfers between devices: 11.4 us -> 0.01 us  [padded(): before = lax.ppermute(last, axis, up)]
    ppermute x1, waiting for transfers between devices: 0.85 us -> 10.5 us  [padded(): after = lax.ppermute(first, axis, down)]
  transfers between devices with their start and end apart: 6 -> 13, of which waited for: 4 -> 5; matrix products, arithmetic and copies ran while one was open for 4% -> 6% of each run, Pallas kernels for 0% -> 0%
where the time goes in v1:
time: 953 us; the launch traced here: 951 us
  waiting for transfers between devices  387 us (41%)
  blocking collectives  233 us (24%)
  local copies, waits for them, and re-layouts  160 us (17%)
  other arithmetic  68.4 us (7%)
  matrix products  51.6 us (5%)
  starting transfers between devices  36.3 us (4%)
  between operations  13.6 us (1%)
    psum x1, waiting for transfers between devices, from_root(): return lax.psum(block, axis)  228 us
    all_gather x2, blocking collectives, combined_all(): everything = jax.tree.map(lambda part: lax.all_gather(part, axis), array)  219 us
    reduce_scatter x1, waiting for transfers between devices, local(): lax.psum_scatter(jnp.dot(attention, output_weight, preferred_element_type...  127 us
    while x24, local copies, waits for them, and re-layouts  69.3 us
    ppermute x7, starting transfers between devices, step_on_side(): block_next = lax.ppermute(d_next, mesh_name, kept_arr)  27.1 us
    sub x2, other arithmetic, attend(): block_scores - block_max  23 us
    ppermute x7, waiting for transfers between devices, step_on_side(): block_next = lax.ppermute(d_next, mesh_name, kept_arr)  21.2 us
    dot_general x2, matrix products, attend(): jnp.einsum('bqhd,bkhd->bhqk', query_heads, group_keys, preferred_element_...  19.3 us
  transfers between devices with their start and end apart: 13, of which 5 were waited for; matrix products, arithmetic and copies ran while one was open for 6% of the time, Pallas kernels for 0%

profile of v1, /device:TPU:0, one launch (start us, length us, event | category | flops | bytes accessed | tf_op | source)
XLA Modules:
  0.0 951.3 jit_solution(9368376471155318311)
XLA Ops:
  8.9 13.6 %all_to_all.17 = s32[8,1,8]{2,1,0:T(1,128)S(1)} all-to-all(s32[8,1,8]{2,1,0:T(1,128)S(1)} %bitcast.228), channel_id=1, replica_groups=mesh['seq'=8,'head'=4] {'seq'}, dimensions={0} | all-to-all | bytes 512 | tf_op jit(solution)/shard_map/all_to_all | solution.py:106
  22.6 7.3 gather_fusion
  29.8 5.5 gather_fusion.2
  35.4 11.8 %broadcast_select_fusion = (bf16[8,8,64,1024]{3,2,1,0:T(8,128)(2,1)}, bf16[8,8,64,1024]{3,2,1,0:T(8,128)(2,1)}) fusion(bf16[8,8,64,1024]{3,2,1,0:T(8,128)(2,1)} %bitcast.215, pred[8,8]{1,0:T(8,128)(4,1)S(1)} %compare_and_fusion, bf16[8,8,64,1024]{3,2,1,0:T(8,128)(2,1)} %bitcast.214), kind=kLoop, calls=%fused_computation.61 | loop fusion | flops 8388608 | bytes 33554496 | tf_op jit(solution)/shard_map/jit(_take)/select_n | solution.py:107
  47.2 5.2 all-to-all-start.1
  55.0 228.3 %all-reduce.2.cloned.1.call-done = bf16[3,128,1024]{1,2,0:T(8,128)(2,1)} async-done(((bf16[3,128,1024]{1,2,0:T(8,128)(2,1)}), bf16[3,128,1024]{1,2,0:T(8,128)(2,1)}) %all-reduce.2.cloned.1.call-update) | async-done | bytes 786448 | tf_op jit(solution)/shard_map/psum | solution.py:63
  294.2 6.3 dynamic-slice_bitcast_fusion.6
  310.0 10.5 %collective-permute-done.1 = bf16[1,2,64,1024]{3,2,1,0:T(8,128)(2,1)S(1)} collective-permute-done((bf16[1,2,64,1024]{3,2,1,0:T(8,128)(2,1)S(1)}, bf16[1,2,64,1024]{3,2,1,0:T(8,128)(2,1)S(1)}, u32[]{:S(2)}, u32[]{:S(2)}) %collective-permute-start.1) | collective-permute-done | bytes 262176 | tf_op jit(solution)/shard_map/ppermute | solution.py:56
  323.8 19.9 %collective-permute-done.2 = bf16[1,1,8,64,1024]{4,3,2,0,1:T(8,128)(2,1)} collective-permute-done((bf16[1,1,8,64,1024]{4,3,2,0,1:T(8,128)(2,1)}, bf16[1,1,8,64,1024]{4,3,2,0,1:T(8,128)(2,1)}, u32[]{:S(2)}, u32[]{:S(2)}) %collective-permute-start.2) | collective-permute-done | bytes 1048608 | tf_op jit(solution)/shard_map/ppermute | solution.py:42
  348.5 17.5 %collective-permute-start.8 = (bf16[1,1,8,64,1024]{4,3,2,0,1:T(8,128)(2,1)S(1)}, bf16[1,1,8,64,1024]{4,3,2,0,1:T(8,128)(2,1)}, u32[]{:S(2)}, u32[]{:S(2)}) collective-permute-start(bf16[1,1,8,64,1024]{4,3,2,0,1:T(8,128)(2,1)S(1)} %get-tuple-element.463), channel_id=1, source_target_pairs={{0,28},{4,0},{8,4},{12,8},{16,12},{20,16},{24,20},{28,24},{1,29},{... | collective-permute-start | bytes 3145736 | tf_op jit(solution)/shard_map/ppermute | solution.py:42
  367.0 188.5 %all-gather.1 = f32[64,128]{1,0:T(8,128)S(1)} all-gather(f32[8,128]{1,0:T(8,128)S(1)} %fusion.37), channel_id=3, replica_groups=mesh['seq'=8,'head'=4] {'seq'}, dimensions={0}, use_global_device_ids=true | all-gather | bytes 36864 | tf_op jit(solution)/shard_map/all_gather | solution.py:67
  555.4 31.0 %all-gather = f32[64,128]{1,0:T(8,128)S(1)} all-gather(f32[8,128]{1,0:T(8,128)S(1)} %get-tuple-element.487), channel_id=2, replica_groups=mesh['seq'=8,'head'=4] {'seq'}, dimensions={0}, use_global_device_ids=true | all-gather | bytes 36864 | tf_op jit(solution)/shard_map/all_gather | solution.py:67
  606.1 8.4 gather_fusion.1
  615.6 11.0 %while.33 = (s32[]{:T(128)}, f32[8,128]{1,0:T(8,128)S(1)}, f32[8,128]{1,0:T(8,128)S(1)}, f32[8,128,128]{2,1,0:T(8,128)S(1)}, f32[8,8,128]{2,1,0:T(8,128)S(1)}, /...) while((s32[]{:T(128)}, f32[8,128]{1,0:T(8,128)S(1)}, ...), condition=%wide.region_4.5_spmd, body=%wide.region_3.4_spmd.sunk | while | flops 399365 | bytes 1613975 | solution.py:73
  627.5 8.4 gather_fusion.3
  635.9 10.4 %broadcast_select_fusion.2 = (bf16[48,64,1024]{2,1,0:T(8,128)(2,1)}, bf16[48,64,1024]{2,1,0:T(8,128)(2,1)}) fusion(bf16[48,64,1024]{2,1,0:T(8,128)(2,1)} %gather_fusion.3, pred[48]{0:T(512)(128)(4,1)S(1)} %get-tuple-element.453, bf16[48,64,1024]{2,1,0:T(8,128)(2,1)} %gather_fusion.1), kind=kLoop, calls=%fused_computation.63 | loop fusion | flops 6291456 | bytes 25165872 | tf_op jit(solution)/shard_map/jit(_take)/select_n | solution.py:113
  646.3 146.6 %while.34 = (s32[]{:T(128)}, bf16[2,512,1024]{2,1,0:T(8,128)(2,1)}, s32[2]{0:T(128)S(1)}, bf16[18,64,1024]{2,1,0:T(8,128)(2,1)S(1)}, bf16[2,8,3,64,1024]{4,3,2,1...) while((s32[]{:T(128)}, bf16[2,512,1024]{2,1,0:T(8,128)(2,1)}, ...), condition=%wide.region_11.14_spmd.clone.clone, body=%wide.region_8.13_spmd.clone.clone.sunk | while | flops 1091585536 | bytes 126397792 | solution.py:218
  657.5 6.7 bitcast_dynamic-update-slice_fusion.3
  666.8 8.9 copy.127
  676.1 9.7 %fusion.93 = f32[8,8,64,512]{3,2,1,0:T(8,128)} fusion(bf16[8,512,8,128]{3,2,1,0:T(8,128)(2,1)} %bitcast.201, bf16[8,64,8,128]{3,2,1,0:T(8,128)(2,1)S(1)} %bitcast.204), kind=kOutput, calls=%fused_computation.16.clone.1 | convolution fusion | flops 536870912 | bytes 17825792 | tf_op jit(solution)/shard_map/while/body/eval_jaxpr/bqhd,bkhd->bhqk/dot_general | solution.py:191
  685.9 11.5 %fusion.96 = (f32[8,8,64]{2,1,0:T(8,128)S(1)}, bf16[8,8,64,512]{3,2,1,0:T(8,128)(2,1)}) fusion(f32[8,8,64,512]{3,2,1,0:T(8,128)} %fusion.93, pred[8,512]{1,0:T(8,128)(4,1)S(1)} %or_and_fusion.2), kind=kOutput, calls=%fused_computation.125.clone.1 | output fusion | flops 16777728 | bytes 12603392 | tf_op jit(solution)/shard_map/while/body/eval_jaxpr/sub | solution.py:203
  699.9 8.8 copy.126
  708.7 6.6 fusion.97
  730.8 6.7 bitcast_dynamic-update-slice_fusion.3
  740.1 8.9 copy.127
  749.4 9.7 %fusion.93 = f32[8,8,64,512]{3,2,1,0:T(8,128)} fusion(bf16[8,512,8,128]{3,2,1,0:T(8,128)(2,1)} %bitcast.201, bf16[8,64,8,128]{3,2,1,0:T(8,128)(2,1)S(1)} %bitcast.204), kind=kOutput, calls=%fused_computation.16.clone.1 | convolution fusion | flops 536870912 | bytes 17825792 | tf_op jit(solution)/shard_map/while/body/eval_jaxpr/bqhd,bkhd->bhqk/dot_general | solution.py:191
  759.2 11.5 %fusion.96 = (f32[8,8,64]{2,1,0:T(8,128)S(1)}, bf16[8,8,64,512]{3,2,1,0:T(8,128)(2,1)}) fusion(f32[8,8,64,512]{3,2,1,0:T(8,128)} %fusion.93, pred[8,512]{1,0:T(8,128)(4,1)S(1)} %or_and_fusion.2), kind=kOutput, calls=%fused_computation.125.clone.1 | output fusion | flops 16777728 | bytes 12603392 | tf_op jit(solution)/shard_map/while/body/eval_jaxpr/sub | solution.py:203
  773.2 8.8 copy.126
  782.0 6.6 fusion.97
  798.3 16.1 %fusion.45 = f32[1024,4096]{1,0:T(8,128)} fusion(bf16[1024,4096]{1,0:T(8,128)(2,1)} %param.19, bf16[896,1024]{0,1:T(8,128)(2,1)} %copy.92, bf16[128,1024]{0,1:T(8,128)(2,1)S(1)} %bitcast_select_fusion), kind=kOutput, calls=%fused_computation.77 | convolution fusion | flops 8594128896 | bytes 27262976 | tf_op jit(solution)/shard_map/dot_general | solution.py:224
  814.4 126.5 %reduce-scatter.2.cloned.1.call-done = f32[256,4096]{1,0:T(8,128)} async-done(((f32[1024,4096]{1,0:T(8,128)}), f32[256,4096]{1,0:T(8,128)}) %reduce-scatter.2.cloned.1.call-update) | async-done | bytes 4194320 | tf_op jit(solution)/shard_map/reduce_scatter | solution.py:223
  940.9 3.8 convert_element_type.51
  (142 shorter events, 112.5 us)
Async XLA Ops:
  22.5 7.3 copy-start
  47.2 6.2 slice-start
  47.2 580.3 %all-to-all-start.1 = ((bf16[8,8,64,1024]{3,2,1,0:T(8,128)(2,1)}), bf16[8,8,64,1024]{3,2,1,0:T(8,128)(2,1)}, u32[]{:S(2)}, u32[]{:S(2)}) async-start(bf16[8,8,64,1024]{3,2,1,0:T(8,128)(2,1)} %get-tuple-element.481), calls=%async_computation.1 | async-start | bytes 16777216 | tf_op jit(solution)/shard_map/all_to_all | solution.py:109
  52.3 231.0 %all-reduce.2.cloned.1.call-start = ((), (), s32[]{:S(2)}) async-start(), calls=%async_computation.3 | async-start | bytes 1572864 | tf_op jit(solution)/shard_map/psum | solution.py:63
  54.9 559.5 %all-gather.5.cloned.1.call-start = ((), (), s32[]{:S(2)}) async-start(), calls=%async_computation.5 | async-start | bytes 4718592 | tf_op jit(solution)/shard_map/all_gather | solution.py:67
  283.3 5.0 copy-start.1
  286.3 2.0 copy-start.2
  290.4 650.6 %reduce-scatter.2.cloned.1.call-start = ((), (), s32[]{:S(2)}) async-start(), calls=%async_computation.4 | async-start | bytes 20971520 | tf_op jit(solution)/shard_map/reduce_scatter | solution.py:223
  291.5 16.6 %collective-permute-start = (bf16[1,2,64,1024]{3,2,1,0:T(8,128)(2,1)S(1)}, bf16[1,2,64,1024]{3,2,1,0:T(8,128)(2,1)S(1)}, u32[]{:S(2)}, u32[]{:S(2)}) collective-permute-start(bf16[1,2,64,1024]{3,2,1,0:T(8,128)(2,1)S(1)} %maximum_bitcast_fusion), channel_id=1, source_target_pairs={{0,4},{4,8},{8,12},{12,16},{16,20},{20,24},{24,28},{1,5},{5,9},{9,... | collective-permute-start | bytes 786440 | tf_op jit(solution)/shard_map/ppermute | solution.py:55
  300.5 43.2 %collective-permute-start.2 = (bf16[1,1,8,64,1024]{4,3,2,0,1:T(8,128)(2,1)}, bf16[1,1,8,64,1024]{4,3,2,0,1:T(8,128)(2,1)}, u32[]{:S(2)}, u32[]{:S(2)}) collective-permute-start(bf16[1,1,8,64,1024]{4,3,2,0,1:T(8,128)(2,1)} %get-tuple-element.469), channel_id=1, source_target_pairs={{0,4},{4,8},{8,12},{12,16},{16,20},{20,24},{24,28},{28,0},{1,5},{5... | collective-permute-start | bytes 3145736 | tf_op jit(solution)/shard_map/ppermute | solution.py:42
  301.9 18.6 %collective-permute-start.1 = (bf16[1,2,64,1024]{3,2,1,0:T(8,128)(2,1)S(1)}, bf16[1,2,64,1024]{3,2,1,0:T(8,128)(2,1)S(1)}, u32[]{:S(2)}, u32[]{:S(2)}) collective-permute-start(bf16[1,2,64,1024]{3,2,1,0:T(8,128)(2,1)S(1)} %maximum_bitcast_fusion.1), channel_id=1, source_target_pairs={{4,0},{8,4},{12,8},{16,12},{20,16},{24,20},{28,24},{5,1},{9,5},{13... | collective-permute-start | bytes 786440 | tf_op jit(solution)/shard_map/ppermute | solution.py:56
  303.2 45.4 %collective-permute-start.3 = (bf16[1,1,8,64,1024]{4,3,2,0,1:T(8,128)(2,1)}, bf16[1,1,8,64,1024]{4,3,2,0,1:T(8,128)(2,1)}, u32[]{:S(2)}, u32[]{:S(2)}) collective-permute-start(bf16[1,1,8,64,1024]{4,3,2,0,1:T(8,128)(2,1)} %get-tuple-element.468), channel_id=1, source_target_pairs={{0,8},{4,12},{8,16},{12,20},{16,24},{20,28},{24,0},{28,4},{1,9},{5... | collective-permute-start | bytes 3145736 | tf_op jit(solution)/shard_map/ppermute | solution.py:42
  307.0 59.0 %copy-start.3 = (f32[8,128,1024]{2,1,0:T(8,128)S(1)}, f32[8,128,1024]{2,1,0:T(8,128)}, u32[]{:S(2)}) copy-start(f32[8,128,1024]{2,1,0:T(8,128)} %copy-done.2) | copy-start | bytes 12582916
  307.0 287.7 %collective-permute-start.4 = (bf16[1,1,8,64,1024]{4,3,2,0,1:T(8,128)(2,1)}, bf16[1,1,8,64,1024]{4,3,2,0,1:T(8,128)(2,1)}, u32[]{:S(2)}, u32[]{:S(2)}) collective-permute-start(bf16[1,1,8,64,1024]{4,3,2,0,1:T(8,128)(2,1)} %get-tuple-element.467), channel_id=1, source_target_pairs={{0,12},{4,16},{8,20},{12,24},{16,28},{20,0},{24,4},{28,8},{1,13},{... | collective-permute-start | bytes 3145736 | tf_op jit(solution)/shard_map/ppermute | solution.py:42
  308.1 288.9 %collective-permute-start.5 = (bf16[1,1,8,64,1024]{4,3,2,0,1:T(8,128)(2,1)}, bf16[1,1,8,64,1024]{4,3,2,0,1:T(8,128)(2,1)}, u32[]{:S(2)}, u32[]{:S(2)}) collective-permute-start(bf16[1,1,8,64,1024]{4,3,2,0,1:T(8,128)(2,1)} %get-tuple-element.466), channel_id=1, source_target_pairs={{0,16},{4,20},{8,24},{12,28},{16,0},{20,4},{24,8},{28,12},{1,17},{... | collective-permute-start | bytes 3145736 | tf_op jit(solution)/shard_map/ppermute | solution.py:42
  320.4 278.8 %collective-permute-start.6 = (bf16[1,1,8,64,1024]{4,3,2,0,1:T(8,128)(2,1)}, bf16[1,1,8,64,1024]{4,3,2,0,1:T(8,128)(2,1)}, u32[]{:S(2)}, u32[]{:S(2)}) collective-permute-start(bf16[1,1,8,64,1024]{4,3,2,0,1:T(8,128)(2,1)} %get-tuple-element.465), channel_id=1, source_target_pairs={{0,20},{4,24},{8,28},{12,0},{16,4},{20,8},{24,12},{28,16},{1,21},{... | collective-permute-start | bytes 3145736 | tf_op jit(solution)/shard_map/ppermute | solution.py:42
  343.7 257.9 %collective-permute-start.7 = (bf16[1,1,8,64,1024]{4,3,2,0,1:T(8,128)(2,1)}, bf16[1,1,8,64,1024]{4,3,2,0,1:T(8,128)(2,1)}, u32[]{:S(2)}, u32[]{:S(2)}) collective-permute-start(bf16[1,1,8,64,1024]{4,3,2,0,1:T(8,128)(2,1)} %get-tuple-element.464), channel_id=1, source_target_pairs={{0,24},{4,28},{8,0},{12,4},{16,8},{20,12},{24,16},{28,20},{1,25},{... | collective-permute-start | bytes 3145736 | tf_op jit(solution)/shard_map/ppermute | solution.py:42
  348.5 255.3 %collective-permute-start.8 = (bf16[1,1,8,64,1024]{4,3,2,0,1:T(8,128)(2,1)S(1)}, bf16[1,1,8,64,1024]{4,3,2,0,1:T(8,128)(2,1)}, u32[]{:S(2)}, u32[]{:S(2)}) collective-permute-start(bf16[1,1,8,64,1024]{4,3,2,0,1:T(8,128)(2,1)S(1)} %get-tuple-element.463), channel_id=1, source_target_pairs={{0,28},{4,0},{8,4},{12,8},{16,12},{20,16},{24,20},{28,24},{1,29},{... | collective-permute-start | bytes 3145736 | tf_op jit(solution)/shard_map/ppermute | solution.py:42
  666.8 8.9 copy-start.4
  740.1 8.9 copy-start.4
  792.9 5.3 copy-start.5
Sparse Core Ops, SparseCore 0:
  56.6 226.7 all-reduce.1
  290.5 202.8 all-gather.4
  814.5 126.3 reduce-scatter.1
